TPU v7x, 8 devices: a whole 2x2x1 slice. The times are simulated.
8 devices in a mesh: f: 2 (over z, y), h: 4 (over x, core).
Axes of the slice: x: 2, y: 2, z: 1, core: 2. Of those that a mesh axis runs over, the one named last changes fastest.
Arguments:
- x: bfloat16 [512, 4096], P(None, 'h')
- g1: float32 [4096], P('h')
- g2: float32 [4096], P('h')
- w_gate: bfloat16 [4096, 14336], P('h', 'f')
- w_up: bfloat16 [4096, 14336], P('h', 'f')
- w_down: bfloat16 [14336, 4096], P('f', 'h')
- o: bfloat16 [512, 4096], P(None, 'f')
- w_o: bfloat16 [4096, 4096], P('f', 'h')
- w_qkv: bfloat16 [4096, 6144], P('h', 'f')
Outputs:
- output 1: bfloat16 [512, 4096], P(None, 'h')
- output 2: bfloat16 [512, 6144], P(None, 'f')
All inputs are finite; a program needn't handle non-finite values.
Results may differ from a plain program's by a relative error of at most 0.00394098.
Values are sent between devices in bfloat16 or wider.
A program may use at most 1 GiB of HBM per device.

v0:
```python
import jax
import jax.numpy as jnp
from jax import lax
from jax.sharding import PartitionSpec as P

EPS = 1e-6


def _dot(a, b):
    return jnp.dot(a, b, preferred_element_type=jnp.float32)


def _norm(x, g, d):
    xf = x.astype(jnp.float32)
    ss = lax.psum(jnp.sum(xf * xf, axis=-1, keepdims=True), 'h')
    r = lax.rsqrt(ss / d + EPS)
    return (xf * r * g).astype(jnp.bfloat16)


def solution(mesh):
    h = mesh.shape['h']

    def body(x, g1, g2, w_gate, w_up, w_down, o, w_o, w_qkv):
        d = x.shape[1] * h
        n = _norm(x, g1, d)
        gt, up = lax.psum((_dot(n, w_gate), _dot(n, w_up)), 'h')
        a = (jax.nn.silu(gt) * up).astype(jnp.bfloat16)
        y = lax.psum(_dot(a, w_down) + _dot(o, w_o), 'f')
        x_next = (x.astype(jnp.float32) + y).astype(jnp.bfloat16)
        n1 = _norm(x_next, g2, d)
        qkv = lax.psum(_dot(n1, w_qkv), 'h').astype(jnp.bfloat16)
        return x_next, qkv

    in_specs = (P(None, 'h'), P('h'), P('h'), P('h', 'f'), P('h', 'f'), P('f', 'h'),
                P(None, 'f'), P('f', 'h'), P('h', 'f'))
    return jax.shard_map(body, mesh=mesh, in_specs=in_specs,
                         out_specs=(P(None, 'h'), P(None, 'f')), check_vma=False)
```

profile of v0, /device:TPU:0, one launch (start us, length us, event | category | flops | bytes accessed | tf_op | source)
XLA Modules:
  0.0 746.0 jit_solution(13566548311548074331)
XLA Ops:
  7.2 0.0 copy-start
  7.2 0.0 all-reduce.7.cloned.1.call-start
  7.2 1.6 fusion.4
  8.9 8.7 %psum.42 = f32[512,1]{0,1:T(1,128)S(1)} all-reduce(f32[512,1]{0,1:T(1,128)S(1)} %bitcast.11), channel_id=1, replica_groups=mesh['f'=2,'h'=4] {'h'}, use_global_device_ids=true, to_apply=%region_1.0 | all-reduce | flops 512 | bytes 4096 | tf_op jit(solution)/shard_map/psum | solution.py:15
  17.6 0.0 copy-start.2
  17.6 0.0 copy-start.3
  17.6 0.0 copy-start.4
  17.7 16.5 %fusion.13 = f32[512,7168]{1,0:T(8,128)} fusion(bf16[1024,7168]{1,0:T(8,128)(2,1)} %param.13, bf16[512,1024]{1,0:T(8,128)(2,1)} %param.9, f32[1024]{0:T(1024)} %param.10, f32[512]{0:T(512)S(1)} %bitcast.12), kind=kOutput, calls=%fused_computation.18 | convolution fusion | flops 7518289920 | bytes 30414848 | tf_op jit(solution)/shard_map/dot_general | solution.py:10
  34.1 0.0 copy-done.2
  34.1 0.0 copy-done.3
  34.1 0.0 copy-done.4
  34.2 11.1 %fusion.15 = f32[512,7168]{1,0:T(8,128)} fusion(bf16[1024,7168]{1,0:T(8,128)(2,1)S(1)} %copy-done.3, bf16[512,1024]{1,0:T(8,128)(2,1)S(1)} %copy-done.2, f32[1024]{0:T(1024)S(1)} %copy-done.4, f32[512]{0:T(512)S(1)} %bitcast.13), kind=kOutput, calls=%fused_computation.19 | convolution fusion | flops 7518289920 | bytes 30414848 | tf_op jit(solution)/shard_map/dot_general | solution.py:10
  45.2 0.0 all-reduce.7.cloned.1.call-update
  45.3 0.0 all-reduce.5.cloned.1.call-start
  45.3 0.0 copy-done
  45.3 5.8 fusion.19
  51.2 479.0 %all-reduce.7.cloned.1.call-done = (f32[512,7168]{1,0:T(8,128)}, f32[512,7168]{1,0:T(8,128)}) async-done(((f32[512,7168]{1,0:T(8,128)}, f32[512,7168]{1,0:T(8,128)}), (f32[512,7168]{1,0:T(8,128)}, f32[512,7168]{1,0:T(8,128)})) %all-reduce.7.cloned.1.call-update) | async-done | bytes 29360144 | tf_op jit(solution)/shard_map/psum | solution.py:26
  530.2 21.1 %fusion.8 = f32[512,1024]{1,0:T(8,128)} fusion(f32[512,1024]{1,0:T(8,128)} %fusion.19, bf16[7168,1024]{1,0:T(8,128)(2,1)} %param.14, f32[512,7168]{1,0:T(8,128)} %get-tuple-element.2, f32[512,7168]{1,0:T(8,128)} %get-tuple-element.3), kind=kOutput, calls=%fused_computation.14 | convolution fusion | flops 7538737152 | bytes 48234496 | tf_op jit(solution)/shard_map/dot_general | solution.py:10
  551.3 0.0 copy-start.5
  551.3 0.0 all-reduce.5.cloned.1.call-update
  551.3 57.5 %all-reduce.5.cloned.1.call-done = f32[512,1024]{1,0:T(8,128)} async-done(((f32[512,1024]{1,0:T(8,128)}), f32[512,1024]{1,0:T(8,128)}) %all-reduce.5.cloned.1.call-update) | async-done | bytes 2097168 | tf_op jit(solution)/shard_map/psum | solution.py:28
  608.9 2.9 fusion.1
  611.7 6.5 psum.46
  618.2 0.0 copy-done.5
  618.2 0.0 copy-start.1
  618.2 9.4 %fusion.9 = f32[512,3072]{1,0:T(8,128)} fusion(bf16[1024,3072]{1,0:T(8,128)(2,1)} %param.17, bf16[512,1024]{1,0:T(8,128)(2,1)} %get-tuple-element.5, f32[1024]{0:T(1024)S(1)} %copy-done.5, f32[512]{0:T(512)S(1)} %bitcast.14), kind=kOutput, calls=%fused_computation.15 | convolution fusion | flops 3223322624 | bytes 13637632 | tf_op jit(solution)/shard_map/dot_general | solution.py:10
  627.6 111.5 %all-reduce.8 = bf16[512,3072]{1,0:T(8,128)(2,1)} all-reduce(f32[512,3072]{1,0:T(8,128)} %fusion.9), channel_id=1, replica_groups=mesh['f'=2,'h'=4] {'h'}, use_global_device_ids=true, to_apply=%region_7.8 | all-reduce | flops 1572864 | bytes 9437184 | tf_op jit(solution)/shard_map/psum | solution.py:31
  739.1 0.0 copy-done.1
  (2 shorter events, 0.0 us)
Async XLA Ops:
  7.2 38.1 %copy-start = (bf16[512,2048]{1,0:T(8,128)(2,1)S(1)}, bf16[512,2048]{1,0:T(8,128)(2,1)}, u32[]{:S(2)}) copy-start(bf16[512,2048]{1,0:T(8,128)(2,1)} %param.15) | copy-start | bytes 6291460
  7.2 523.0 %all-reduce.7.cloned.1.call-start = ((), (), s32[]{:S(2)}) async-start(), calls=%async_computation.1 | async-start | bytes 58720256 | tf_op jit(solution)/shard_map/psum | solution.py:26
  17.6 16.5 %copy-start.2 = (bf16[512,1024]{1,0:T(8,128)(2,1)S(1)}, bf16[512,1024]{1,0:T(8,128)(2,1)}, u32[]{:S(2)}) copy-start(bf16[512,1024]{1,0:T(8,128)(2,1)} %param.9) | copy-start | bytes 3145732
  17.6 16.5 %copy-start.3 = (bf16[1024,7168]{1,0:T(8,128)(2,1)S(1)}, bf16[1024,7168]{1,0:T(8,128)(2,1)}, u32[]{:S(2)}) copy-start(bf16[1024,7168]{1,0:T(8,128)(2,1)} %param.12) | copy-start | bytes 44040196
  17.6 16.5 %copy-start.4 = (f32[1024]{0:T(1024)S(1)}, f32[1024]{0:T(1024)}, u32[]{:S(2)}) copy-start(f32[1024]{0:T(1024)} %param.10) | copy-start | bytes 12292
  45.3 563.6 %all-reduce.5.cloned.1.call-start = ((), (), s32[]{:S(2)}) async-start(), calls=%async_computation | async-start | bytes 4194304 | tf_op jit(solution)/shard_map/psum | solution.py:28
  551.3 66.9 %copy-start.5 = (f32[1024]{0:T(1024)S(1)}, f32[1024]{0:T(1024)}, u32[]{:S(2)}) copy-start(f32[1024]{0:T(1024)} %param.11) | copy-start | bytes 12292
  618.2 120.9 %copy-start.1 = (bf16[512,2048]{1,0:T(8,128)(2,1)S(1)}, bf16[512,2048]{1,0:T(8,128)(2,1)}, u32[]{:S(2)}) copy-start(bf16[512,2048]{1,0:T(8,128)(2,1)} %param.15) | copy-start | bytes 6291460
Sparse Core Ops, SparseCore 0:
  45.4 484.7 all-reduce.6
  551.4 57.3 all-reduce.4
where the time goes:
time: 746 us
  waiting for transfers between devices  537 us (72%)
  blocking collectives  127 us (17%)
  matrix products  63.9 us (9%)
  between operations  14.1 us (2%)
    psum x1, waiting for transfers between devices, body(): gt, up = lax.psum((_dot(n, w_gate), _dot(n, w_up)), 'h')  479 us
    psum x1, blocking collectives, body(): qkv = lax.psum(_dot(n1, w_qkv), 'h').astype(jnp.bfloat16)  112 us
    dot_general x5, matrix products, _dot(): return jnp.dot(a, b, preferred_element_type=jnp.float32)  63.9 us
    psum x1, waiting for transfers between devices, body(): y = lax.psum(_dot(a, w_down) + _dot(o, w_o), 'f')  57.5 us
    psum x2, blocking collectives, _norm(): ss = lax.psum(jnp.sum(xf * xf, axis=-1, keepdims=True), 'h')  15.2 us
  transfers between devices with their start and end apart: 2, of which 2 were waited for; matrix products, arithmetic and copies ran while one was open for 1% of the time, Pallas kernels for 0%

commit v1 on v0

v1 whole, which is shorter than its diff:
```python
import functools

import jax
import jax.numpy as jnp
from jax import lax
from jax.experimental import pallas as pl
from jax.experimental.pallas import tpu as pltpu
from jax.sharding import PartitionSpec as P

EPS = 1e-6
MESH = pl.DeviceIdType.MESH
F32 = jnp.float32
BF16 = jnp.bfloat16
NT = 256
NB = 3


def _dot(a, b):
    return jnp.dot(a, b, preferred_element_type=F32)


def _kernel(T, C, d,
            x_hbm, g1_hbm, g2_hbm, wg_hbm, wu_hbm, wd_hbm, o_hbm, wo_hbm, wq_hbm,
            xo_hbm, qo_hbm, wsib_hbm,
            xv, g1v, g2v, ov, wd, wo, wq, wbuf, nf, ss1, psnd, prcv, pkeep, abuf, ysnd, yrcv, xov, ss2, nf2,
            qsnd, qrcv, qkeep, qall,
            in_sem, ld_sem, ws_s, ws_r, wq_s, wq_r, n_s, n_r, ss1_s, ss1_r, p_s, p_r, a_s, a_r, y_s, y_r, ss2_s, ss2_r,
            n2_s, n2_r, q_s, q_r, qa_s, qa_r, out_sem):
    S = xv.shape[0]
    HL = xv.shape[1]
    FB = abuf.shape[3]
    QB = qall.shape[3]
    TP = FB // NT
    QT = QB // NT
    DT = HL // NT
    f = lax.axis_index('f')
    h = lax.axis_index('h')
    c = lax.rem(h, 2)
    xx = h // 2
    hx = (1 - xx) * 2 + c
    hs = xx * 2 + (1 - c)
    hd = (1 - xx) * 2 + (1 - c)
    XP, SIB, DIAG, YP = (f, hx), (f, hs), (f, hd), (1 - f, h)

    def rcopy(src, dst, s, r, dev):
        return pltpu.make_async_remote_copy(src_ref=src, dst_ref=dst, send_sem=s, recv_sem=r, device_id=dev,
                                            device_id_type=MESH)

    def lcopy(src, dst, s):
        return pltpu.make_async_copy(src, dst, s)

    def mo(v, m):
        return pl.multiple_of(v, m)

    first = [lcopy(x_hbm, xv, in_sem.at[0]), lcopy(g1_hbm, g1v, in_sem.at[1]), lcopy(g2_hbm, g2v, in_sem.at[2])]
    for cp in first:
        cp.start()

    bar = pltpu.get_barrier_semaphore()
    for dev in (XP, SIB, DIAG, YP):
        pl.semaphore_signal(bar, inc=1, device_id=dev, device_id_type=MESH)
    pl.semaphore_wait(bar, 4)

    def wcopy(t, m):
        blk = jnp.where(t < TP, hd, hs)
        col = mo(blk * FB + lax.rem(t, TP) * NT, NT)
        src = (wg_hbm, wu_hbm)[m].at[:, pl.ds(col, NT)]
        return rcopy(src, wsib_hbm.at[t, m], ws_s.at[t, m], ws_r.at[t, m], SIB)

    def wqcopy(b, t):
        blk = (hd, hs)[b]
        col = mo(blk * QB + t * NT, NT)
        return rcopy(wq_hbm.at[:, pl.ds(col, NT)], wq.at[b, t, pl.ds(HL, HL)], wq_s.at[b, t], wq_r.at[b, t], SIB)

    for m in range(2):
        wcopy(jnp.int32(0), m).start()
    for cp in first:
        cp.wait()

    for j in range(S // 128):
        xf = xv[pl.ds(j * 128, 128), :].astype(F32)
        s = jnp.sum(xf * xf, axis=1, keepdims=True)
        ss1[h, :, pl.ds(j * 128, 128)] = jnp.broadcast_to(s, (128, 128)).T[0:8]

    def ss1copy(k):
        dev = (XP, SIB, DIAG)[k]
        return rcopy(ss1.at[h], ss1.at[h], ss1_s.at[k], ss1_r.at[k], dev)

    for k in range(3):
        ss1copy(k).start()
    for k in range(3):
        ss1copy(k).wait()
    r1 = lax.rsqrt((ss1[0] + ss1[1] + ss1[2] + ss1[3]) / d + EPS)
    for j in range(S // 128):
        rr = jnp.broadcast_to(r1[0:1, j * 128:(j + 1) * 128], (128, 128)).T
        for l in range(HL // 128):
            xf = xv[pl.ds(j * 128, 128), pl.ds(l * 128, 128)].astype(F32)
            nf[pl.ds(j * 128, 128), pl.ds(l * 128, 128)] = (xf * rr * g1v[:, pl.ds(l * 128, 128)]).astype(BF16)
    ncp = rcopy(nf.at[:, pl.ds(0, HL)], nf.at[:, pl.ds(HL, HL)], n_s, n_r, SIB)
    ncp.start()

    @pl.loop(1, 2 * TP)
    def _(t):
        for m in range(2):
            wcopy(t, m).start()

    for b in range(2):
        for t in range(QT):
            wqcopy(b, t).start()

    def loads(g):
        t = lax.rem(g, 2 * TP)
        bs = lax.rem(g, NB)
        blk = jnp.where(t < TP, hx, h)
        col = mo(blk * FB + lax.rem(t, TP) * NT, NT)
        return (lcopy(wg_hbm.at[:, pl.ds(col, NT)], wbuf.at[bs, 0, pl.ds(0, HL)], ld_sem.at[bs, 0]),
                lcopy(wu_hbm.at[:, pl.ds(col, NT)], wbuf.at[bs, 1, pl.ds(0, HL)], ld_sem.at[bs, 1]),
                lcopy(wsib_hbm.at[t, 0], wbuf.at[bs, 0, pl.ds(HL, HL)], ld_sem.at[bs, 2]),
                lcopy(wsib_hbm.at[t, 1], wbuf.at[bs, 1, pl.ds(HL, HL)], ld_sem.at[bs, 3]))

    def start_load(g):
        cps = loads(g)
        cps[0].start()
        cps[1].start()

        @pl.when(g < 2 * TP)
        def _():
            for m in range(2):
                wcopy(g, m).wait_recv()

        cps[2].start()
        cps[3].start()

    def pcopy(j, t):
        s2 = lax.rem(j, 2)
        s3 = lax.rem(j, 3)
        return rcopy(psnd.at[s2, t], prcv.at[s3, t], p_s.at[s2, t], p_r.at[s3, t], XP)

    def gu(j, t):
        g = j * (2 * TP) + t
        bs = lax.rem(g, NB)
        for cp in loads(g):
            cp.wait()

        @pl.when(g + NB - 1 < C * 2 * TP)
        def _():
            start_load(g + NB - 1)

        nn = nf[pl.ds(mo(j * T, T), T), :]
        return _dot(nn, wbuf[bs, 0]), _dot(nn, wbuf[bs, 1])

    def s12(j):
        s2 = lax.rem(j, 2)

        @pl.loop(0, TP)
        def _(t):
            @pl.when(j >= 2)
            def _():
                pcopy(j - 2, t).wait_send()

            gg, uu = gu(j, t)
            psnd[s2, t, :, 0:NT] = gg
            psnd[s2, t, :, NT:2 * NT] = uu
            pcopy(j, t).start()

        @pl.loop(0, TP)
        def _(t):
            gg, uu = gu(j, t + TP)
            pkeep[s2, t, :, 0:NT] = gg
            pkeep[s2, t, :, NT:2 * NT] = uu

    def acopy(i, k):
        s2 = lax.rem(i, 2)
        if k == 0:
            return rcopy(abuf.at[s2, h], abuf.at[s2, h], a_s.at[s2, 0], a_r.at[s2, 0], XP)
        if k == 1:
            return rcopy(abuf.at[s2, h], abuf.at[s2, h], a_s.at[s2, 1], a_r.at[s2, 1], SIB)
        return rcopy(abuf.at[s2, hx], abuf.at[s2, hx], a_s.at[s2, 2], a_r.at[s2, 2], SIB)

    def s3(i):
        s2 = lax.rem(i, 2)
        sl3 = lax.rem(i, 3)

        @pl.loop(0, TP)
        def _(t):
            pcopy(i, t).wait_recv()
            gg = pkeep[s2, t, :, 0:NT] + prcv[sl3, t, :, 0:NT]
            uu = pkeep[s2, t, :, NT:2 * NT] + prcv[sl3, t, :, NT:2 * NT]
            abuf[s2, h, :, pl.ds(mo(t * NT, NT), NT)] = (gg * jax.nn.sigmoid(gg) * uu).astype(BF16)

        acopy(i, 0).start()
        acopy(i, 1).start()

    def ycopy(i):
        s2 = lax.rem(i, 2)
        return rcopy(ysnd.at[s2], yrcv.at[i], y_s.at[s2], y_r.at[i], YP)

    def s4(i):
        s2 = lax.rem(i, 2)
        acopy(i, 0).wait_recv()
        acopy(i, 2).start()
        acopy(i, 1).wait_recv()
        acopy(i, 2).wait_recv()

        @pl.loop(0, DT)
        def _(n):
            acc = _dot(ov[pl.ds(mo(i * T, T), T), :], wo[n])
            for b in range(4):
                acc += _dot(abuf[s2, b], wd[n, b * FB:(b + 1) * FB])
            ysnd[s2, :, pl.ds(mo(n * NT, NT), NT)] = acc

        ycopy(i).start()

    def ss2copy(i, k):
        dev = (XP, SIB, DIAG)[k]
        return rcopy(ss2.at[i, h], ss2.at[i, h], ss2_s.at[i, k], ss2_r.at[i, k], dev)

    def xocopy(i):
        rows = pl.ds(mo(i * T, T), T)
        return lcopy(xov.at[rows], xo_hbm.at[rows], out_sem.at[i, 4])

    def s5(i):
        s2 = lax.rem(i, 2)
        for k in range(3):
            acopy(i, k).wait_send()
        ycopy(i).wait()
        rows = pl.ds(mo(i * T, T), T)
        xn = (xv[rows, :].astype(F32) + (ysnd[s2] + yrcv[i])).astype(BF16)
        xov[rows, :] = xn
        xf = xn.astype(F32)
        s = jnp.broadcast_to(jnp.sum(xf * xf, axis=1, keepdims=True), (T, 128))
        if T < 128:
            s = jnp.concatenate([s] * (128 // T), axis=0)
        ss2[i, h] = s.T[0:8]
        for k in range(3):
            ss2copy(i, k).start()
        xocopy(i).start()

    def n2copy(i):
        rows = pl.ds(mo(i * T, T), T)
        return rcopy(nf2.at[rows, pl.ds(0, HL)], nf2.at[rows, pl.ds(HL, HL)], n2_s.at[i], n2_r.at[i], SIB)

    def s6(i):
        rows = pl.ds(mo(i * T, T), T)
        for k in range(3):
            ss2copy(i, k).wait_recv()
        r = lax.rsqrt((ss2[i, 0] + ss2[i, 1] + ss2[i, 2] + ss2[i, 3]) / d + EPS)
        rr = jnp.broadcast_to(r[0:1], (128, 128)).T[0:T]
        for l in range(HL // 128):
            xf = xov[rows, pl.ds(l * 128, 128)].astype(F32)
            nf2[rows, pl.ds(l * 128, 128)] = (xf * rr * g2v[:, pl.ds(l * 128, 128)]).astype(BF16)
        n2copy(i).start()

    def qcopy(i):
        return rcopy(qsnd.at[i], qrcv.at[i], q_s.at[i], q_r.at[i], XP)

    def s7(i):
        n2copy(i).wait_recv()
        nn = nf2[pl.ds(mo(i * T, T), T), :]
        for t in range(QT):
            qsnd[i, :, t * NT:(t + 1) * NT] = _dot(nn, wq[0, t])
        qcopy(i).start()
        for t in range(QT):
            qkeep[i, :, t * NT:(t + 1) * NT] = _dot(nn, wq[1, t])

    def qacopy(i, k):
        b = (h, h, hx)[k]
        dev = (XP, SIB, SIB)[k]
        return rcopy(qall.at[i, b], qall.at[i, b], qa_s.at[i, k], qa_r.at[i, k], dev)

    def s8(i):
        qcopy(i).wait_recv()
        qall[i, h] = (qkeep[i] + qrcv[i]).astype(BF16)
        qacopy(i, 0).start()
        qacopy(i, 1).start()

    def qocopy(i, b):
        return lcopy(qall.at[i, b], qo_hbm.at[pl.ds(mo(i * T, T), T), pl.ds(b * QB, QB)], out_sem.at[i, b])

    def s9(i):
        qacopy(i, 0).wait_recv()
        qacopy(i, 2).start()
        qacopy(i, 1).wait_recv()
        qacopy(i, 2).wait_recv()
        for b in range(4):
            qocopy(i, b).start()

    ncp.wait_recv()
    for g in range(NB - 1):
        start_load(jnp.int32(g))

    res = [lcopy(o_hbm, ov, in_sem.at[3])]
    for n in range(DT):
        res.append(lcopy(wd_hbm.at[:, pl.ds(n * NT, NT)], wd.at[n], in_sem.at[4 + n]))
        res.append(lcopy(wo_hbm.at[:, pl.ds(n * NT, NT)], wo.at[n], in_sem.at[4 + DT + n]))
    for b in range(2):
        blk = (hx, h)[b]
        for t in range(QT):
            res.append(lcopy(wq_hbm.at[:, pl.ds(mo(blk * QB + t * NT, NT), NT)], wq.at[b, t, pl.ds(0, HL)],
                             in_sem.at[4 + 2 * DT + b * QT + t]))

    @pl.loop(0, 2)
    def _(j):
        s12(j)

        @pl.when(j == 0)
        def _():
            for cp in res:
                cp.start()

    for cp in res:
        cp.wait()
    for b in range(2):
        for t in range(QT):
            wqcopy(b, t).wait()

    def stage(fn, i):
        @pl.when((i >= 0) & (i < C))
        def _():
            fn(i)

    @pl.loop(0, C + 3)
    def _(i):
        stage(s3, i)
        stage(s12, i + 2)
        stage(s5, i - 1)
        stage(s4, i)
        stage(s6, i - 1)
        stage(s8, i - 2)
        stage(s7, i - 1)
        stage(s9, i - 3)

    ncp.wait_send()

    @pl.loop(0, 2 * TP)
    def _(t):
        for m in range(2):
            wcopy(t, m).wait_send()

    @pl.loop(0, TP)
    def _(t):
        pcopy(C - 2, t).wait_send()
        pcopy(C - 1, t).wait_send()

    @pl.loop(0, C)
    def _(i):
        for k in range(3):
            ss2copy(i, k).wait_send()
            qacopy(i, k).wait_send()
        n2copy(i).wait_send()
        qcopy(i).wait_send()
        xocopy(i).wait()
        for b in range(4):
            qocopy(i, b).wait()


def solution(mesh):
    nh = mesh.shape['h']

    def body(x, g1, g2, w_gate, w_up, w_down, o, w_o, w_qkv):
        S, HL = x.shape
        FL = w_gate.shape[1]
        FB = FL // nh
        QL = w_qkv.shape[1]
        QB = QL // nh
        OL = o.shape[1]
        T = 64
        C = S // T
        TP, QT, DT = FB // NT, QB // NT, HL // NT
        d = HL * nh
        any_ = pl.BlockSpec(memory_space=pl.ANY)
        dma = pltpu.SemaphoreType.DMA
        V = pltpu.VMEM
        scratch = [
            V((S, HL), BF16), V((1, HL), F32), V((1, HL), F32), V((S, OL), BF16),
            V((DT, FL, NT), BF16), V((DT, OL, NT), BF16), V((2, QT, 2 * HL, NT), BF16),
            V((NB, 2, 2 * HL, NT), BF16), V((S, 2 * HL), BF16), V((nh, 8, S), F32),
            V((2, TP, T, 2 * NT), F32), V((3, TP, T, 2 * NT), F32), V((2, TP, T, 2 * NT), F32),
            V((2, nh, T, FB), BF16), V((2, T, HL), F32), V((C, T, HL), F32), V((S, HL), BF16),
            V((C, nh, 8, 128), F32), V((S, 2 * HL), BF16),
            V((C, T, QB), F32), V((C, T, QB), F32), V((C, T, QB), F32), V((C, nh, T, QB), BF16),
            dma((4 + 2 * DT + 2 * QT,)), dma((NB, 4)), dma((2 * TP, 2)), dma((2 * TP, 2)), dma((2, QT)), dma((2, QT)),
            dma, dma, dma((3,)), dma((3,)), dma((2, TP)), dma((3, TP)), dma((2, 3)), dma((2, 3)), dma((2,)), dma((C,)),
            dma((C, 3)), dma((C, 3)), dma((C,)), dma((C,)), dma((C,)), dma((C,)), dma((C, 3)), dma((C, 3)),
            dma((C, 5)),
        ]
        xo, qo, _ = pl.pallas_call(
            functools.partial(_kernel, T, C, float(d)),
            out_shape=(jax.ShapeDtypeStruct((S, HL), BF16), jax.ShapeDtypeStruct((S, QL), BF16),
                       jax.ShapeDtypeStruct((2 * TP, 2, HL, NT), BF16)),
            in_specs=[any_] * 9,
            out_specs=(any_, any_, any_),
            scratch_shapes=scratch,
            compiler_params=pltpu.CompilerParams(collective_id=0, has_side_effects=True, vmem_limit_bytes=67043328),
            name='block',
        )(x, g1.reshape(1, HL), g2.reshape(1, HL), w_gate, w_up, w_down, o, w_o, w_qkv)
        return xo, qo

    in_specs = (P(None, 'h'), P('h'), P('h'), P('h', 'f'), P('h', 'f'), P('f', 'h'),
                P(None, 'f'), P('f', 'h'), P('h', 'f'))
    return jax.shard_map(body, mesh=mesh, in_specs=in_specs,
                         out_specs=(P(None, 'h'), P(None, 'f')), check_vma=False)
```

time: 746 us -> 310 us (0.42)
  waiting for transfers between devices: 537 us -> 0 us
  Pallas kernels: 0 us -> 302 us
  blocking collectives: 127 us -> 0 us
  matrix products: 63.9 us -> 0 us
  between operations: 14.1 us -> 0.64 us
    psum x2 -> x0, waiting for transfers between devices: 537 us -> none  [the longest x1 479 us: body(): gt, up = lax.psum((_dot(n, w_gate), _dot(n, w_up)), 'h')]
    pallas_call x0 -> x1, Pallas kernels: none -> 302 us  [body(): pl.pallas_call(functools.partial(_kernel, T, C, float(d)), out_shape=(jax...]
    psum x3 -> x0, blocking collectives: 127 us -> none  [the longest x1 112 us: body(): qkv = lax.psum(_dot(n1, w_qkv), 'h').astype(jnp.bfloat16)]
    dot_general x5 -> x0, matrix products: 63.9 us -> none  [_dot(): return jnp.dot(a, b, preferred_element_type=jnp.float32)]
  transfers between devices with their start and end apart: 2 -> 0, of which waited for: 2 -> 0; matrix products, arithmetic and copies ran while one was open for 1% -> 0% of each run, Pallas kernels for 0% -> 0%
where the time goes in v1:
time: 310 us; the launch traced here: 309 us
  Pallas kernels  302 us (97%)
  local copies, waits for them, and re-layouts  6.02 us (2%)
    pallas_call x1, Pallas kernels, body(): pl.pallas_call(functools.partial(_kernel, T, C, float(d)), out_shape=(jax...  302 us

profile of v1, /device:TPU:0, one launch (start us, length us, event | category | flops | bytes accessed | tf_op | source)
XLA Modules:
  0.0 308.8 jit_solution(15857281654360049191)
XLA Ops:
  0.6 302.1 %block.1 = (bf16[512,1024]{1,0:T(8,128)(2,1)}, bf16[512,3072]{1,0:T(8,128)(2,1)}, bf16[14,2,1024,256]{3,2,1,0:T(8,128)(2,1)}) custom-call(bf16[512,1024]{1,0:T(8,128)(2,1)} %x_hbm.1, f32[1,1024]{1,0:T(1,128)} %bitcast.2, f32[1,1024]{1,0:T(1,128)} %bitcast.3, bf16[1024,7168]{1,0:T(8,128)(2,1)} %wg_hbm.1, bf16[1024,7168]{1,0:T(8,128)(2,1)} %wu_hbm.1, ...), custom_call_target="tpu_custom_call" | custom-call | tf_op jit(solution)/shard_map/block/pallas_call | solution.py:387
  302.8 2.3 copy.13
  305.1 3.8 %copy.14 = bf16[512,3072]{1,0:T(8,128)(2,1)} copy(bf16[512,3072]{1,0:T(8,128)(2,1)} %get-tuple-element.9) | data formatting | bytes 6291456

commit v2 on v1

v2 whole, which is shorter than its diff:
```python
import functools

import jax
import jax.numpy as jnp
from jax import lax
from jax.experimental import pallas as pl
from jax.experimental.pallas import tpu as pltpu
from jax.sharding import PartitionSpec as P

EPS = 1e-6
MESH = pl.DeviceIdType.MESH
F32 = jnp.float32
BF16 = jnp.bfloat16
NT = 256
NB = 3


def _dot(a, b):
    return jnp.dot(a, b, preferred_element_type=F32)


def _kernel(T, C, d,
            x_hbm, g1_hbm, g2_hbm, wg_hbm, wu_hbm, wd_hbm, o_hbm, wo_hbm, wq_hbm,
            xov, qall, wsib_hbm,
            xv, g1v, g2v, ov, wd, wo, wq, wbuf, nf, ss1, psnd, prcv, pkeep, abuf, ysnd, yrcv, ss2, nf2,
            qsnd, qrcv, qkeep,
            in_sem, ld_sem, ws_s, ws_r, wq_s, wq_r, n_s, n_r, ss1_s, ss1_r, p_s, p_r, a_s, a_r, y_s, y_r, ss2_s, ss2_r,
            n2_s, n2_r, q_s, q_r, qa_s, qa_r):
    S = xv.shape[0]
    HL = xv.shape[1]
    FB = abuf.shape[3]
    QB = qsnd.shape[2]
    TP = FB // NT
    QT = QB // NT
    DT = HL // NT
    f = lax.axis_index('f')
    h = lax.axis_index('h')
    c = lax.rem(h, 2)
    xx = h // 2
    hx = (1 - xx) * 2 + c
    hs = xx * 2 + (1 - c)
    hd = (1 - xx) * 2 + (1 - c)
    XP, SIB, DIAG, YP = (f, hx), (f, hs), (f, hd), (1 - f, h)

    def rcopy(src, dst, s, r, dev):
        return pltpu.make_async_remote_copy(src_ref=src, dst_ref=dst, send_sem=s, recv_sem=r, device_id=dev,
                                            device_id_type=MESH)

    def lcopy(src, dst, s):
        return pltpu.make_async_copy(src, dst, s)

    def lwait(ref, sem):
        lcopy(ref, ref, sem).wait()

    def rwait(ref, sem):
        rcopy(ref, ref, sem, sem, XP).wait_recv()

    def mo(v, m):
        return pl.multiple_of(v, m)

    first = [lcopy(x_hbm, xv, in_sem.at[0]), lcopy(g1_hbm, g1v.at[:, pl.ds(0, HL)], in_sem.at[1]),
             lcopy(g2_hbm, g2v, in_sem.at[2])]
    for cp in first:
        cp.start()

    bar = pltpu.get_barrier_semaphore()
    for dev in (XP, SIB, DIAG, YP):
        pl.semaphore_signal(bar, inc=1, device_id=dev, device_id_type=MESH)

    NL = 3 * TP + (C - 2) * 2 * TP

    def tile_of(g):
        return jnp.where(g < TP, g, lax.rem(g + TP, 2 * TP))

    def own(g):
        t = tile_of(g)
        bs = lax.rem(g, NB)
        blk = jnp.where(t < TP, hx, h)
        col = mo(blk * FB + lax.rem(t, TP) * NT, NT)
        return (lcopy(wg_hbm.at[:, pl.ds(col, NT)], wbuf.at[bs, 0, pl.ds(0, HL)], ld_sem.at[bs]),
                lcopy(wu_hbm.at[:, pl.ds(col, NT)], wbuf.at[bs, 1, pl.ds(0, HL)], ld_sem.at[bs]))

    def sib(g):
        t = tile_of(g)
        bs = lax.rem(g, NB)
        return (lcopy(wsib_hbm.at[t, 0], wbuf.at[bs, 0, pl.ds(HL, HL)], ld_sem.at[bs]),
                lcopy(wsib_hbm.at[t, 1], wbuf.at[bs, 1, pl.ds(HL, HL)], ld_sem.at[bs]))

    def wcopy(t, m):
        blk = jnp.where(t < TP, hd, hs)
        col = mo(blk * FB + lax.rem(t, TP) * NT, NT)
        src = (wg_hbm, wu_hbm)[m].at[:, pl.ds(col, NT)]
        return rcopy(src, wsib_hbm.at[t, m], ws_s, ws_r.at[t], SIB)

    def wqcopy(b, t):
        blk = (hd, hs)[b]
        col = mo(blk * QB + t * NT, NT)
        return rcopy(wq_hbm.at[:, pl.ds(col, NT)], wq.at[b, t, pl.ds(HL, HL)], wq_s, wq_r, SIB)

    def start_sib(g):
        @pl.when((g < TP) | ((g >= 2 * TP) & (g < 3 * TP)))
        def _():
            t = tile_of(g)
            rwait(wsib_hbm.at[t], ws_r.at[t])

        for cp in sib(g):
            cp.start()

    def start_own(g):
        for cp in own(g):
            cp.start()

    def wait_tile(g):
        bs = lax.rem(g, NB)
        lwait(wbuf.at[bs], ld_sem.at[bs])

    for g in range(2):
        start_own(jnp.int32(g))
    for cp in first:
        cp.wait()

    R0 = 128
    for j in range(S // 128):
        xf = xv[pl.ds(j * 128, 128), :].astype(F32)
        s = jnp.sum(xf * xf, axis=1, keepdims=True)
        ss1[j, h] = jnp.broadcast_to(s, (128, 128)).T[0:1]

    def ss1copy(j, k):
        dev = (XP, SIB, DIAG)[k]
        return rcopy(ss1.at[j, h], ss1.at[j, h], ss1_s, ss1_r.at[min(j, 1)], dev)

    def xcopy(k):
        rows = (pl.ds(0, R0), pl.ds(R0, S - R0))[k]
        return rcopy(xv.at[rows], nf2.at[rows, pl.ds(HL, HL)], n_s.at[k], n_r.at[k], SIB)

    gcp = rcopy(g1v.at[:, pl.ds(0, HL)], g1v.at[:, pl.ds(HL, HL)], n_s.at[2], n_r.at[2], SIB)

    pl.semaphore_wait(bar, 4)
    for k in (0, 2, 1):
        ss1copy(0, k).start()
    xcopy(0).start()
    gcp.start()
    for m in range(2):
        wcopy(jnp.int32(0), m).start()
    for j in range(1, S // 128):
        for k in range(3):
            ss1copy(j, k).start()
    xcopy(1).start()

    @pl.loop(1, 2 * TP)
    def _(t):
        for m in range(2):
            wcopy(t, m).start()

    for b in range(2):
        for t in range(QT):
            wqcopy(b, t).start()


    def norm1(j):
        if j == 0:
            rwait(ss1.at[0, pl.ds(0, 3)], ss1_r.at[0])
        elif j == 1:
            rwait(ss1.at[pl.ds(1, S // 128 - 1), pl.ds(0, 3)], ss1_r.at[1])
        r1 = lax.rsqrt((ss1[j, 0] + ss1[j, 1] + ss1[j, 2] + ss1[j, 3]) / d + EPS)
        rr = jnp.broadcast_to(r1, (128, 128)).T
        rows = pl.ds(j * 128, 128)
        for half in range(2):
            for l in range(HL // 128):
                cols = pl.ds(half * HL + l * 128, 128)
                xb = xv[rows, pl.ds(l * 128, 128)] if half == 0 else nf2[rows, cols]
                nf[rows, cols] = (xb.astype(F32) * rr * g1v[:, cols]).astype(BF16)

    rwait(wsib_hbm.at[0], ws_r.at[0])
    for cp in sib(jnp.int32(0)):
        cp.start()
    gcp.wait_recv()
    xcopy(0).wait_recv()
    norm1(0)

    def pcopy(j, t):
        s2 = lax.rem(j, 2)
        s3 = lax.rem(j, 3)
        return rcopy(psnd.at[s2, t], prcv.at[s3, t], p_s.at[s2], p_r.at[s3], XP)

    def gu(g, row, n):
        bs = lax.rem(g, NB)
        nn = nf[pl.ds(row, n), :]
        return _dot(nn, wbuf[bs, 0]), _dot(nn, wbuf[bs, 1])

    def prefetch(g):
        @pl.when(g < NL)
        def _():
            start_own(g)
            start_sib(g)

    def put_send(j, t, gg, uu):
        s2 = lax.rem(j, 2)
        psnd[s2, t, :, 0:NT] = gg
        psnd[s2, t, :, NT:2 * NT] = uu
        pcopy(j, t).start()

    def s12(j):
        s2 = lax.rem(j, 2)
        g0 = 3 * TP + (j - 2) * (2 * TP)
        rwait(psnd.at[s2], p_s.at[s2])
        row = mo(j * T, T)

        @pl.loop(0, TP)
        def _(t):
            wait_tile(g0 + t)
            prefetch(g0 + t + NB - 1)
            gg, uu = gu(g0 + t, row, T)
            put_send(j, t, gg, uu)

        @pl.loop(0, TP)
        def _(t):
            wait_tile(g0 + t + TP)
            prefetch(g0 + t + TP + NB - 1)
            gg, uu = gu(g0 + t + TP, row, T)
            pkeep[s2, t, :, 0:NT] = gg
            pkeep[s2, t, :, NT:2 * NT] = uu

    def acopy(i, k):
        sl = lax.rem(i, 3)
        b = (h, h, hx)[k]
        return rcopy(abuf.at[sl, b], abuf.at[sl, b], a_s.at[sl, k], a_r.at[sl, k], (XP, SIB, SIB)[k])

    def s3(i):
        s2 = lax.rem(i, 2)
        sl = lax.rem(i, 3)

        rwait(prcv.at[sl], p_r.at[sl])

        @pl.loop(0, TP)
        def _(t):
            gg = pkeep[s2, t, :, 0:NT] + prcv[sl, t, :, 0:NT]
            uu = pkeep[s2, t, :, NT:2 * NT] + prcv[sl, t, :, NT:2 * NT]
            abuf[sl, h, :, pl.ds(mo(t * NT, NT), NT)] = (gg * jax.nn.sigmoid(gg) * uu).astype(BF16)

        acopy(i, 0).start()
        acopy(i, 1).start()

    def ycopy(i, n):
        s2 = lax.rem(i, 2)
        cols = pl.ds(mo(n * NT, NT), NT)
        sl = lax.rem(i, 3)
        return rcopy(ysnd.at[s2, :, cols], yrcv.at[sl, :, cols], y_s.at[s2], y_r.at[sl], YP)

    def down(sl, b, n):
        return _dot(abuf[sl, b], wd[n, pl.ds(mo(b * FB, FB), FB)])

    def s4a(i):
        s2 = lax.rem(i, 2)
        sl = lax.rem(i, 3)
        acopy(i, 1).wait_recv()

        @pl.loop(0, DT)
        def _(n):
            acc = _dot(ov[pl.ds(mo(i * T, T), T), :], wo[n])
            acc += down(sl, h, n)
            acc += down(sl, hs, n)
            ysnd[s2, :, pl.ds(mo(n * NT, NT), NT)] = acc

    def s4b(i):
        s2 = lax.rem(i, 2)
        sl = lax.rem(i, 3)
        acopy(i, 0).wait_recv()
        acopy(i, 2).start()
        acopy(i, 2).wait_recv()

        @pl.loop(0, DT)
        def _(n):
            ysnd[s2, :, pl.ds(mo(n * NT, NT), NT)] += down(sl, hx, n) + down(sl, hd, n)
            ycopy(i, n).start()

    def ss2copy(i, k):
        dev = (XP, SIB, DIAG)[k]
        return rcopy(ss2.at[i, h], ss2.at[i, h], ss2_s, ss2_r.at[i], dev)

    def s5(i):
        s2 = lax.rem(i, 2)
        for k in range(3):
            acopy(i, k).wait_send()
        sl = lax.rem(i, 3)
        rwait(ysnd.at[s2], y_s.at[s2])
        rwait(yrcv.at[sl], y_r.at[sl])
        rows = pl.ds(mo(i * T, T), T)
        xn = (xv[rows, :].astype(F32) + (ysnd[s2] + yrcv[sl])).astype(BF16)
        xov[rows, :] = xn
        xf = xn.astype(F32)
        s = jnp.broadcast_to(jnp.sum(xf * xf, axis=1, keepdims=True), (T, 128))
        if T < 128:
            s = jnp.concatenate([s] * (128 // T), axis=0)
        ss2[i, h] = s.T[0:1]
        for k in range(3):
            ss2copy(i, k).start()

    def n2copy(i):
        rows = pl.ds(mo(i * T, T), T)
        return rcopy(nf2.at[rows, pl.ds(0, HL)], nf2.at[rows, pl.ds(HL, HL)], n2_s, n2_r.at[i], SIB)

    def s6(i):
        rows = pl.ds(mo(i * T, T), T)
        rwait(ss2.at[i, pl.ds(0, 3)], ss2_r.at[i])
        r = lax.rsqrt((ss2[i, 0] + ss2[i, 1] + ss2[i, 2] + ss2[i, 3]) / d + EPS)
        rr = jnp.broadcast_to(r, (128, 128)).T[0:T]
        for l in range(HL // 128):
            xf = xov[rows, pl.ds(l * 128, 128)].astype(F32)
            nf2[rows, pl.ds(l * 128, 128)] = (xf * rr * g2v[:, pl.ds(l * 128, 128)]).astype(BF16)
        n2copy(i).start()

    def qcopy(i):
        return rcopy(qsnd.at[i], qrcv.at[i], q_s, q_r.at[i], XP)

    def s7(i):
        n2copy(i).wait_recv()
        nn = nf2[pl.ds(mo(i * T, T), T), :]
        for t in range(QT):
            qsnd[i, :, t * NT:(t + 1) * NT] = _dot(nn, wq[0, t])
        qcopy(i).start()
        for t in range(QT):
            qkeep[i, :, t * NT:(t + 1) * NT] = _dot(nn, wq[1, t])

    def qacopy(i, k):
        b = (h, h, hx)[k]
        dev = (XP, SIB, SIB)[k]
        blk = qall.at[pl.ds(mo(i * T, T), T), pl.ds(mo(b * QB, NT), QB)]
        return rcopy(blk, blk, qa_s, qa_r.at[i if k == 0 else C], dev)

    def s8(i):
        qcopy(i).wait_recv()
        for t in range(QT):
            cols = pl.ds(t * NT, NT)
            qall[pl.ds(mo(i * T, T), T), pl.ds(mo(h * QB + t * NT, NT), NT)] = (qkeep[i, :, cols] + qrcv[i, :, cols]).astype(BF16)
        qacopy(i, 0).start()
        qacopy(i, 1).start()

    def s9a(i):
        qacopy(i, 0).wait_recv()
        qacopy(i, 2).start()

    @pl.loop(0, TP)
    def _(t):
        wait_tile(t)
        gg, uu = gu(t, 0, T)
        put_send(jnp.int32(0), t, gg, uu)
        start_own(t + 2)
        start_sib(t + 1)

    start_sib(jnp.int32(TP + 1))

    @pl.loop(0, TP)
    def _(t):
        wait_tile(TP + t)
        prefetch(TP + t + NB - 1)
        gg, uu = gu(TP + t, T, T)
        put_send(jnp.int32(1), t, gg, uu)

    xcopy(1).wait_recv()
    for j in range(1, S // 128):
        norm1(j)

    res = [[] for _ in range(4)]
    for n in range(DT):
        res[n % 4].append(lcopy(wd_hbm.at[:, pl.ds(n * NT, NT)], wd.at[n], in_sem.at[4]))
        res[n % 4].append(lcopy(wo_hbm.at[:, pl.ds(n * NT, NT)], wo.at[n], in_sem.at[5]))
    res[0].append(lcopy(o_hbm, ov, in_sem.at[3]))
    for b in range(2):
        blk = (hx, h)[b]
        for t in range(QT):
            res[3].append(lcopy(wq_hbm.at[:, pl.ds(mo(blk * QB + t * NT, NT), NT)], wq.at[b, t, pl.ds(0, HL)],
                                in_sem.at[6]))

    @pl.loop(0, TP)
    def _(t):
        wait_tile(2 * TP + t)
        prefetch(2 * TP + t + NB - 1)
        for k in range(4):
            @pl.when(t == k)
            def _(k=k):
                for cp in res[k]:
                    cp.start()

        gg, uu = gu(2 * TP + t, 0, 2 * T)
        for j in range(2):
            pkeep[j, t, :, 0:NT] = gg[j * T:(j + 1) * T]
            pkeep[j, t, :, NT:2 * NT] = uu[j * T:(j + 1) * T]

    def stage(fn, i, lo=0):
        @pl.when((i >= lo) & (i < C))
        def _():
            fn(i)

    def loaded():
        lwait(ov, in_sem.at[3])
        lwait(wd, in_sem.at[4])
        lwait(wo, in_sem.at[5])
        lwait(wq.at[:, :, pl.ds(0, HL)], in_sem.at[6])
        rwait(wq.at[:, :, pl.ds(HL, HL)], wq_s)
        rwait(wq.at[:, :, pl.ds(HL, HL)], wq_r)

    @pl.loop(0, C - 2)
    def _(i):
        s3(i)
        s12(i + 2)

        @pl.when(i == 0)
        def _():
            loaded()

        stage(s5, i - 1)
        s4a(i)
        s4b(i)
        stage(s6, i - 2)

    e = C - 1
    done = {s7: 0, s8: 0, s9a: 0}

    def run(*steps):
        for fn, i in steps:
            fn(jnp.int32(i))

    def nxt(*fns):
        for fn in fns:
            if done[fn] < C:
                fn(jnp.int32(done[fn]))
                done[fn] += 1

    run((s3, e - 1), (s4a, e - 1), (s5, e - 2), (s6, e - 3), (s3, e))
    nxt(s7)
    run((s4b, e - 1))
    nxt(s7)
    run((s4a, e), (s6, e - 2), (s4b, e))
    nxt(s7, s8)
    run((s5, e - 1))
    nxt(s7, s8)
    run((s5, e), (s6, e - 1))
    nxt(s7, s8)
    run((s6, e))
    nxt(s7, s8, s9a, s7, s8, s9a, s7, s8, s9a)
    gcp.wait_send()
    rwait(ss1.at[:, pl.ds(0, 3)], ss1_s)
    for k in range(2):
        xcopy(k).wait_send()

    rwait(wsib_hbm, ws_s)

    for k in range(2):
        rwait(psnd.at[k], p_s.at[k])

    while done[s8] < C:
        nxt(s8, s9a)

    rwait(ss2.at[:, pl.ds(0, 3)], ss2_s)
    rwait(nf2.at[:, pl.ds(0, HL)], n2_s)
    rwait(qsnd, q_s)

    while done[s9a] < C:
        nxt(s9a)
    rwait(qall.at[:, pl.ds(0, 2 * QB)], qa_r.at[C])
    rwait(qall.at[:, pl.ds(0, 3 * QB)], qa_s)


def solution(mesh):
    nh = mesh.shape['h']

    def body(x, g1, g2, w_gate, w_up, w_down, o, w_o, w_qkv):
        S, HL = x.shape
        FL = w_gate.shape[1]
        FB = FL // nh
        QL = w_qkv.shape[1]
        QB = QL // nh
        OL = o.shape[1]
        T = 64
        C = S // T
        TP, QT, DT = FB // NT, QB // NT, HL // NT
        d = HL * nh
        any_ = pl.BlockSpec(memory_space=pl.ANY)
        vm = pl.BlockSpec(memory_space=pltpu.VMEM)
        dma = pltpu.SemaphoreType.DMA
        V = pltpu.VMEM
        scratch = [
            V((S, HL), BF16), V((1, 2 * HL), F32), V((1, HL), F32), V((S, OL), BF16),
            V((DT, FL, NT), BF16), V((DT, OL, NT), BF16), V((2, QT, 2 * HL, NT), BF16),
            V((NB, 2, 2 * HL, NT), BF16), V((S, 2 * HL), BF16), V((S // 128, nh, 1, 128), F32),
            V((2, TP, T, 2 * NT), F32), V((3, TP, T, 2 * NT), F32), V((2, TP, T, 2 * NT), F32),
            V((3, nh, T, FB), BF16), V((2, T, HL), F32), V((3, T, HL), F32),
            V((C, nh, 1, 128), F32), V((S, 2 * HL), BF16),
            V((C, T, QB), F32), V((C, T, QB), F32), V((C, T, QB), F32),
            dma((7,)), dma((NB,)), dma, dma((2 * TP,)), dma, dma,
            dma((3,)), dma((3,)), dma, dma((2,)), dma((2,)), dma((3,)), dma((3, 3)), dma((3, 3)), dma((2,)), dma((3,)),
            dma, dma((C,)), dma, dma((C,)), dma, dma((C,)), dma, dma((C + 1,)),
        ]
        xo, qo, _ = pl.pallas_call(
            functools.partial(_kernel, T, C, float(d)),
            out_shape=(V((S, HL), BF16), V((S, QL), BF16), jax.ShapeDtypeStruct((2 * TP, 2, HL, NT), BF16)),
            in_specs=[any_] * 9,
            out_specs=(vm, vm, any_),
            scratch_shapes=scratch,
            compiler_params=pltpu.CompilerParams(collective_id=0, has_side_effects=True, vmem_limit_bytes=56 * 2**20),
            name='block',
        )(x, g1.reshape(1, HL), g2.reshape(1, HL), w_gate, w_up, w_down, o, w_o, w_qkv)
        return xo, qo

    in_specs = (P(None, 'h'), P('h'), P('h'), P('h', 'f'), P('h', 'f'), P('f', 'h'),
                P(None, 'f'), P('f', 'h'), P('h', 'f'))
    return jax.shard_map(body, mesh=mesh, in_specs=in_specs,
                         out_specs=(P(None, 'h'), P(None, 'f')), check_vma=False)
```

time: 310 us -> 264 us (0.85)
  Pallas kernels: 302 us -> 260 us
  local copies, waits for them, and re-layouts: 6.02 us -> 2.64 us
    pallas_call x1, Pallas kernels: 302 us -> 260 us  [body(): pl.pallas_call(functools.partial(_kernel, T, C, float(d)), out_shape=(V((...]
    unnamed x2, local copies, waits for them, and re-layouts: 6.02 us -> 2.64 us
where the time goes in v2:
time: 264 us; the launch traced here: 263 us
  Pallas kernels  260 us (98%)
  local copies, waits for them, and re-layouts  2.64 us (1%)
    pallas_call x1, Pallas kernels, body(): pl.pallas_call(functools.partial(_kernel, T, C, float(d)), out_shape=(V((...  260 us

profile of v2, /device:TPU:0, one launch (start us, length us, event | category | flops | bytes accessed | tf_op | source)
XLA Modules:
  0.0 263.2 jit_solution(17203544069535856927)
XLA Ops:
  0.6 259.9 %block.1 = (bf16[512,1024]{1,0:T(8,128)(2,1)S(1)}, bf16[512,3072]{1,0:T(8,128)(2,1)S(1)}, bf16[14,2,1024,256]{3,2,1,0:T(8,128)(2,1)}) custom-call(bf16[512,1024]{1,0:T(8,128)(2,1)} %x_hbm.1, f32[1,1024]{1,0:T(1,128)} %bitcast.2, f32[1,1024]{1,0:T(1,128)} %bitcast.3, bf16[1024,7168]{1,0:T(8,128)(2,1)} %wg_hbm.1, bf16[1024,7168]{1,0:T(8,128)(2,1)} %wu_hbm.1, ...), custom_call_target="tpu_custom_call" | custom-call | tf_op jit(solution)/shard_map/block/pallas_call | solution.py:495
  260.5 1.0 copy.13
  261.5 1.7 copy.14

commit v3 on v2

--- a/solution.py
+++ b/solution.py
@@ -24,7 +24,7 @@
             xov, qall, wsib_hbm,
             xv, g1v, g2v, ov, wd, wo, wq, wbuf, nf, ss1, psnd, prcv, pkeep, abuf, ysnd, yrcv, ss2, nf2,
             qsnd, qrcv, qkeep,
-            in_sem, ld_sem, ws_s, ws_r, wq_s, wq_r, n_s, n_r, ss1_s, ss1_r, p_s, p_r, a_s, a_r, y_s, y_r, ss2_s, ss2_r,
+            in_sem, ld_sem, w0_s, w0_r, ws_s, ws_r, wq_s, wq_r, n_s, n_r, ss1_s, ss1_r, p_s, p_r, a_s, a_r, y_s, y_r, ss2_s, ss2_r,
             n2_s, n2_r, q_s, q_r, qa_s, qa_r):
     S = xv.shape[0]
     HL = xv.shape[1]
@@ -58,8 +58,9 @@
     def mo(v, m):
         return pl.multiple_of(v, m)
 
-    first = [lcopy(x_hbm, xv, in_sem.at[0]), lcopy(g1_hbm, g1v.at[:, pl.ds(0, HL)], in_sem.at[1]),
-             lcopy(g2_hbm, g2v, in_sem.at[2])]
+    top, rest = pl.ds(0, T), pl.ds(T, S - T)
+    first = [lcopy(x_hbm.at[top], xv.at[top], in_sem.at[0]), lcopy(g1_hbm, g1v.at[:, pl.ds(0, HL)], in_sem.at[1])]
+    second = [lcopy(x_hbm.at[rest], xv.at[rest], in_sem.at[2]), lcopy(g2_hbm, g2v, in_sem.at[7])]
     for cp in first:
         cp.start()
 
@@ -98,7 +99,7 @@
         return rcopy(wq_hbm.at[:, pl.ds(col, NT)], wq.at[b, t, pl.ds(HL, HL)], wq_s, wq_r, SIB)
 
     def start_sib(g):
-        @pl.when((g < TP) | ((g >= 2 * TP) & (g < 3 * TP)))
+        @pl.when((g <= TP) | ((g >= 2 * TP) & (g < 3 * TP)))
         def _():
             t = tile_of(g)
             rwait(wsib_hbm.at[t], ws_r.at[t])
@@ -114,23 +115,34 @@
         bs = lax.rem(g, NB)
         lwait(wbuf.at[bs], ld_sem.at[bs])
 
-    for g in range(2):
-        start_own(jnp.int32(g))
+    start_own(jnp.int32(0))
+    for cp in second:
+        cp.start()
+    start_own(jnp.int32(1))
     for cp in first:
         cp.wait()
 
-    R0 = 128
-    for j in range(S // 128):
-        xf = xv[pl.ds(j * 128, 128), :].astype(F32)
-        s = jnp.sum(xf * xf, axis=1, keepdims=True)
-        ss1[j, h] = jnp.broadcast_to(s, (128, 128)).T[0:1]
+    def row_sums(xf):
+        s = jnp.broadcast_to(jnp.sum(xf * xf, axis=1, keepdims=True), (T, 128))
+        if T < 128:
+            s = jnp.concatenate([s] * (128 // T), axis=0)
+        return s.T[0:1]
+
+    def row_scales(ss):
+        r = lax.rsqrt((ss[0] + ss[1] + ss[2] + ss[3]) / d + EPS)
+        return jnp.broadcast_to(r, (128, 128)).T[0:T]
+
+    def sums1(j):
+        ss1[j, h] = row_sums(xv[pl.ds(j * T, T), :].astype(F32))
+
+    sums1(0)
 
     def ss1copy(j, k):
         dev = (XP, SIB, DIAG)[k]
         return rcopy(ss1.at[j, h], ss1.at[j, h], ss1_s, ss1_r.at[min(j, 1)], dev)
 
     def xcopy(k):
-        rows = (pl.ds(0, R0), pl.ds(R0, S - R0))[k]
+        rows = (top, rest)[k]
         return rcopy(xv.at[rows], nf2.at[rows, pl.ds(HL, HL)], n_s.at[k], n_r.at[k], SIB)
 
     gcp = rcopy(g1v.at[:, pl.ds(0, HL)], g1v.at[:, pl.ds(HL, HL)], n_s.at[2], n_r.at[2], SIB)
@@ -140,14 +152,29 @@
         ss1copy(0, k).start()
     xcopy(0).start()
     gcp.start()
+    def w0copy(m):
+        src = (wg_hbm, wu_hbm)[m].at[:, pl.ds(mo(hd * FB, NT), NT)]
+        return rcopy(src, wbuf.at[0, m, pl.ds(HL, HL)], w0_s, w0_r, SIB)
+
+    for m in range(2):
+        w0copy(m).start()
+
+    @pl.loop(1, TP)
+    def _(t):
+        for m in range(2):
+            wcopy(t, m).start()
+
     for m in range(2):
         wcopy(jnp.int32(0), m).start()
-    for j in range(1, S // 128):
+    for cp in second:
+        cp.wait()
+    for j in range(1, C):
+        sums1(j)
         for k in range(3):
             ss1copy(j, k).start()
     xcopy(1).start()
 
-    @pl.loop(1, 2 * TP)
+    @pl.loop(TP, 2 * TP)
     def _(t):
         for m in range(2):
             wcopy(t, m).start()
@@ -155,25 +182,20 @@
     for b in range(2):
         for t in range(QT):
             wqcopy(b, t).start()
-
 
     def norm1(j):
         if j == 0:
             rwait(ss1.at[0, pl.ds(0, 3)], ss1_r.at[0])
         elif j == 1:
-            rwait(ss1.at[pl.ds(1, S // 128 - 1), pl.ds(0, 3)], ss1_r.at[1])
-        r1 = lax.rsqrt((ss1[j, 0] + ss1[j, 1] + ss1[j, 2] + ss1[j, 3]) / d + EPS)
-        rr = jnp.broadcast_to(r1, (128, 128)).T
-        rows = pl.ds(j * 128, 128)
+            rwait(ss1.at[pl.ds(1, C - 1), pl.ds(0, 3)], ss1_r.at[1])
+        rr = row_scales(ss1.at[j])
+        rows = pl.ds(j * T, T)
         for half in range(2):
             for l in range(HL // 128):
                 cols = pl.ds(half * HL + l * 128, 128)
                 xb = xv[rows, pl.ds(l * 128, 128)] if half == 0 else nf2[rows, cols]
                 nf[rows, cols] = (xb.astype(F32) * rr * g1v[:, cols]).astype(BF16)
 
-    rwait(wsib_hbm.at[0], ws_r.at[0])
-    for cp in sib(jnp.int32(0)):
-        cp.start()
     gcp.wait_recv()
     xcopy(0).wait_recv()
     norm1(0)
@@ -288,11 +310,7 @@
         rows = pl.ds(mo(i * T, T), T)
         xn = (xv[rows, :].astype(F32) + (ysnd[s2] + yrcv[sl])).astype(BF16)
         xov[rows, :] = xn
-        xf = xn.astype(F32)
-        s = jnp.broadcast_to(jnp.sum(xf * xf, axis=1, keepdims=True), (T, 128))
-        if T < 128:
-            s = jnp.concatenate([s] * (128 // T), axis=0)
-        ss2[i, h] = s.T[0:1]
+        ss2[i, h] = row_sums(xn.astype(F32))
         for k in range(3):
             ss2copy(i, k).start()
 
@@ -303,8 +321,7 @@
     def s6(i):
         rows = pl.ds(mo(i * T, T), T)
         rwait(ss2.at[i, pl.ds(0, 3)], ss2_r.at[i])
-        r = lax.rsqrt((ss2[i, 0] + ss2[i, 1] + ss2[i, 2] + ss2[i, 3]) / d + EPS)
-        rr = jnp.broadcast_to(r, (128, 128)).T[0:T]
+        rr = row_scales(ss2.at[i])
         for l in range(HL // 128):
             xf = xov[rows, pl.ds(l * 128, 128)].astype(F32)
             nf2[rows, pl.ds(l * 128, 128)] = (xf * rr * g2v[:, pl.ds(l * 128, 128)]).astype(BF16)
@@ -340,7 +357,17 @@
         qacopy(i, 0).wait_recv()
         qacopy(i, 2).start()
 
-    @pl.loop(0, TP)
+    lwait(wbuf.at[0, :, pl.ds(0, HL)], ld_sem.at[0])
+    halves = [_dot(nf[top, pl.ds(0, HL)], wbuf[0, m, 0:HL]) for m in range(2)]
+    rwait(wbuf.at[0, :, pl.ds(HL, HL)], w0_r)
+    for m in range(2):
+        cols = pl.ds(m * NT, NT)
+        psnd[0, 0, :, cols] = halves[m] + _dot(nf[top, pl.ds(HL, HL)], wbuf[0, m, HL:2 * HL])
+        rcopy(psnd.at[0, 0, :, cols], prcv.at[0, 0, :, cols], p_s.at[0], p_r.at[0], XP).start()
+    start_own(jnp.int32(2))
+    start_sib(jnp.int32(1))
+
+    @pl.loop(1, TP)
     def _(t):
         wait_tile(t)
         gg, uu = gu(t, 0, T)
@@ -349,6 +376,9 @@
         start_sib(t + 1)
 
     start_sib(jnp.int32(TP + 1))
+    xcopy(1).wait_recv()
+    for j in range(1, C):
+        norm1(j)
 
     @pl.loop(0, TP)
     def _(t):
@@ -357,9 +387,6 @@
         gg, uu = gu(TP + t, T, T)
         put_send(jnp.int32(1), t, gg, uu)
 
-    xcopy(1).wait_recv()
-    for j in range(1, S // 128):
-        norm1(j)
 
     res = [[] for _ in range(4)]
     for n in range(DT):
@@ -445,6 +472,7 @@
         xcopy(k).wait_send()
 
     rwait(wsib_hbm, ws_s)
+    rwait(wbuf.at[0, :, pl.ds(HL, HL)], w0_s)
 
     for k in range(2):
         rwait(psnd.at[k], p_s.at[k])
@@ -460,6 +488,16 @@
         nxt(s9a)
     rwait(qall.at[:, pl.ds(0, 2 * QB)], qa_r.at[C])
     rwait(qall.at[:, pl.ds(0, 3 * QB)], qa_s)
+
+
+def _out_kernel(xv, qv, xo, qo, sem):
+    n = xv.shape[0] // 4
+    cps = [pltpu.make_async_copy(a.at[pl.ds(k * n, n)], b.at[pl.ds(k * n, n)], sem.at[m, k])
+           for m, (a, b) in enumerate(((qv, qo), (xv, xo))) for k in range(4)]
+    for cp in cps:
+        cp.start()
+    for cp in cps:
+        cp.wait()
 
 
 def solution(mesh):
@@ -483,12 +521,12 @@
         scratch = [
             V((S, HL), BF16), V((1, 2 * HL), F32), V((1, HL), F32), V((S, OL), BF16),
             V((DT, FL, NT), BF16), V((DT, OL, NT), BF16), V((2, QT, 2 * HL, NT), BF16),
-            V((NB, 2, 2 * HL, NT), BF16), V((S, 2 * HL), BF16), V((S // 128, nh, 1, 128), F32),
+            V((NB, 2, 2 * HL, NT), BF16), V((S, 2 * HL), BF16), V((C, nh, 1, 128), F32),
             V((2, TP, T, 2 * NT), F32), V((3, TP, T, 2 * NT), F32), V((2, TP, T, 2 * NT), F32),
             V((3, nh, T, FB), BF16), V((2, T, HL), F32), V((3, T, HL), F32),
             V((C, nh, 1, 128), F32), V((S, 2 * HL), BF16),
             V((C, T, QB), F32), V((C, T, QB), F32), V((C, T, QB), F32),
-            dma((7,)), dma((NB,)), dma, dma((2 * TP,)), dma, dma,
+            dma((8,)), dma((NB,)), dma, dma, dma, dma((2 * TP,)), dma, dma,
             dma((3,)), dma((3,)), dma, dma((2,)), dma((2,)), dma((3,)), dma((3, 3)), dma((3, 3)), dma((2,)), dma((3,)),
             dma, dma((C,)), dma, dma((C,)), dma, dma((C,)), dma, dma((C + 1,)),
         ]
@@ -501,7 +539,15 @@
             compiler_params=pltpu.CompilerParams(collective_id=0, has_side_effects=True, vmem_limit_bytes=56 * 2**20),
             name='block',
         )(x, g1.reshape(1, HL), g2.reshape(1, HL), w_gate, w_up, w_down, o, w_o, w_qkv)
-        return xo, qo
+        return pl.pallas_call(
+            _out_kernel,
+            out_shape=(jax.ShapeDtypeStruct((S, HL), BF16), jax.ShapeDtypeStruct((S, QL), BF16)),
+            in_specs=[vm, vm],
+            out_specs=(any_, any_),
+            scratch_shapes=[dma((2, 4))],
+            compiler_params=pltpu.CompilerParams(vmem_limit_bytes=2**20),
+            name='out',
+        )(xo, qo)
 
     in_specs = (P(None, 'h'), P('h'), P('h'), P('h', 'f'), P('h', 'f'), P('f', 'h'),
                 P(None, 'f'), P('f', 'h'), P('h', 'f'))

time: 264 us -> 262 us (level)
  local copies, waits for them, and re-layouts: 2.64 us -> 0 us
where the time goes in v3:
time: 262 us; the launch traced here: 261 us
  Pallas kernels  261 us (100%)
    pallas_call x1, Pallas kernels, body(): pl.pallas_call(functools.partial(_kernel, T, C, float(d)), out_shape=(V((...  259 us

profile of v3, /device:TPU:0, one launch (start us, length us, event | category | flops | bytes accessed | tf_op | source)
XLA Modules:
  0.0 261.4 jit_solution(6398460161739347644)
XLA Ops:
  0.6 258.5 %block.1 = (bf16[512,1024]{1,0:T(8,128)(2,1)S(1)}, bf16[512,3072]{1,0:T(8,128)(2,1)S(1)}, bf16[14,2,1024,256]{3,2,1,0:T(8,128)(2,1)}) custom-call(bf16[512,1024]{1,0:T(8,128)(2,1)} %x_hbm.1, f32[1,1024]{1,0:T(1,128)} %bitcast.2, f32[1,1024]{1,0:T(1,128)} %bitcast.3, bf16[1024,7168]{1,0:T(8,128)(2,1)} %wg_hbm.1, bf16[1024,7168]{1,0:T(8,128)(2,1)} %wu_hbm.1, ...), custom_call_target="tpu_custom_call" | custom-call | tf_op jit(solution)/shard_map/block/pallas_call | solution.py:533
  259.2 2.1 out.1

commit v4 on v3

--- a/solution.py
+++ b/solution.py
@@ -13,6 +13,7 @@
 BF16 = jnp.bfloat16
 NT = 256
 NB = 3
+HOLD = 2
 
 
 def _dot(a, b):
@@ -60,7 +61,7 @@
 
     top, rest = pl.ds(0, T), pl.ds(T, S - T)
     first = [lcopy(x_hbm.at[top], xv.at[top], in_sem.at[0]), lcopy(g1_hbm, g1v.at[:, pl.ds(0, HL)], in_sem.at[1])]
-    second = [lcopy(x_hbm.at[rest], xv.at[rest], in_sem.at[2]), lcopy(g2_hbm, g2v, in_sem.at[7])]
+    second = [lcopy(x_hbm.at[rest], xv.at[rest], in_sem.at[2]), lcopy(g2_hbm, g2v, in_sem.at[3])]
     for cp in first:
         cp.start()
 
@@ -115,12 +116,11 @@
         bs = lax.rem(g, NB)
         lwait(wbuf.at[bs], ld_sem.at[bs])
 
+    first[0].wait()
     start_own(jnp.int32(0))
     for cp in second:
         cp.start()
     start_own(jnp.int32(1))
-    for cp in first:
-        cp.wait()
 
     def row_sums(xf):
         s = jnp.broadcast_to(jnp.sum(xf * xf, axis=1, keepdims=True), (T, 128))
@@ -147,6 +147,7 @@
 
     gcp = rcopy(g1v.at[:, pl.ds(0, HL)], g1v.at[:, pl.ds(HL, HL)], n_s.at[2], n_r.at[2], SIB)
 
+    first[1].wait()
     pl.semaphore_wait(bar, 4)
     for k in (0, 2, 1):
         ss1copy(0, k).start()
@@ -154,7 +155,7 @@
     gcp.start()
     def w0copy(m):
         src = (wg_hbm, wu_hbm)[m].at[:, pl.ds(mo(hd * FB, NT), NT)]
-        return rcopy(src, wbuf.at[0, m, pl.ds(HL, HL)], w0_s, w0_r, SIB)
+        return rcopy(src, wbuf.at[0, m, pl.ds(HL, HL)], w0_s, w0_r.at[m], SIB)
 
     for m in range(2):
         w0copy(m).start()
@@ -246,7 +247,7 @@
     def acopy(i, k):
         sl = lax.rem(i, 3)
         b = (h, h, hx)[k]
-        return rcopy(abuf.at[sl, b], abuf.at[sl, b], a_s.at[sl, k], a_r.at[sl, k], (XP, SIB, SIB)[k])
+        return rcopy(abuf.at[sl, b], abuf.at[sl, b], a_s.at[sl], a_r.at[sl, k], (XP, SIB, SIB)[k])
 
     def s3(i):
         s2 = lax.rem(i, 2)
@@ -298,13 +299,12 @@
 
     def ss2copy(i, k):
         dev = (XP, SIB, DIAG)[k]
-        return rcopy(ss2.at[i, h], ss2.at[i, h], ss2_s, ss2_r.at[i], dev)
+        return rcopy(ss2.at[i, h], ss2.at[i, h], ss2_s, ss2_r.at[lax.rem(i, 4)], dev)
 
     def s5(i):
         s2 = lax.rem(i, 2)
-        for k in range(3):
-            acopy(i, k).wait_send()
         sl = lax.rem(i, 3)
+        rwait(abuf.at[sl, pl.ds(0, 3)], a_s.at[sl])
         rwait(ysnd.at[s2], y_s.at[s2])
         rwait(yrcv.at[sl], y_r.at[sl])
         rows = pl.ds(mo(i * T, T), T)
@@ -320,7 +320,7 @@
 
     def s6(i):
         rows = pl.ds(mo(i * T, T), T)
-        rwait(ss2.at[i, pl.ds(0, 3)], ss2_r.at[i])
+        rwait(ss2.at[i, pl.ds(0, 3)], ss2_r.at[lax.rem(i, 4)])
         rr = row_scales(ss2.at[i])
         for l in range(HL // 128):
             xf = xov[rows, pl.ds(l * 128, 128)].astype(F32)
@@ -345,24 +345,26 @@
         blk = qall.at[pl.ds(mo(i * T, T), T), pl.ds(mo(b * QB, NT), QB)]
         return rcopy(blk, blk, qa_s, qa_r.at[i if k == 0 else C], dev)
 
-    def s8(i):
+    def s8(i, late=False):
         qcopy(i).wait_recv()
         for t in range(QT):
             cols = pl.ds(t * NT, NT)
             qall[pl.ds(mo(i * T, T), T), pl.ds(mo(h * QB + t * NT, NT), NT)] = (qkeep[i, :, cols] + qrcv[i, :, cols]).astype(BF16)
-        qacopy(i, 0).start()
         qacopy(i, 1).start()
+        if late:
+            pl.when(c == 0)(qacopy(i, 0).start)
+        else:
+            qacopy(i, 0).start()
 
     def s9a(i):
         qacopy(i, 0).wait_recv()
         qacopy(i, 2).start()
 
     lwait(wbuf.at[0, :, pl.ds(0, HL)], ld_sem.at[0])
-    halves = [_dot(nf[top, pl.ds(0, HL)], wbuf[0, m, 0:HL]) for m in range(2)]
-    rwait(wbuf.at[0, :, pl.ds(HL, HL)], w0_r)
     for m in range(2):
         cols = pl.ds(m * NT, NT)
-        psnd[0, 0, :, cols] = halves[m] + _dot(nf[top, pl.ds(HL, HL)], wbuf[0, m, HL:2 * HL])
+        rwait(wbuf.at[0, m, pl.ds(HL, HL)], w0_r.at[m])
+        psnd[0, 0, :, cols] = _dot(nf[top, :], wbuf[0, m])
         rcopy(psnd.at[0, 0, :, cols], prcv.at[0, 0, :, cols], p_s.at[0], p_r.at[0], XP).start()
     start_own(jnp.int32(2))
     start_sib(jnp.int32(1))
@@ -390,14 +392,14 @@
 
     res = [[] for _ in range(4)]
     for n in range(DT):
-        res[n % 4].append(lcopy(wd_hbm.at[:, pl.ds(n * NT, NT)], wd.at[n], in_sem.at[4]))
-        res[n % 4].append(lcopy(wo_hbm.at[:, pl.ds(n * NT, NT)], wo.at[n], in_sem.at[5]))
-    res[0].append(lcopy(o_hbm, ov, in_sem.at[3]))
+        res[n % 4].append(lcopy(wd_hbm.at[:, pl.ds(n * NT, NT)], wd.at[n], in_sem.at[1]))
+        res[n % 4].append(lcopy(wo_hbm.at[:, pl.ds(n * NT, NT)], wo.at[n], in_sem.at[2]))
+    res[0].append(lcopy(o_hbm, ov, in_sem.at[0]))
     for b in range(2):
         blk = (hx, h)[b]
         for t in range(QT):
             res[3].append(lcopy(wq_hbm.at[:, pl.ds(mo(blk * QB + t * NT, NT), NT)], wq.at[b, t, pl.ds(0, HL)],
-                                in_sem.at[6]))
+                                in_sem.at[3]))
 
     @pl.loop(0, TP)
     def _(t):
@@ -420,10 +422,10 @@
             fn(i)
 
     def loaded():
-        lwait(ov, in_sem.at[3])
-        lwait(wd, in_sem.at[4])
-        lwait(wo, in_sem.at[5])
-        lwait(wq.at[:, :, pl.ds(0, HL)], in_sem.at[6])
+        lwait(ov, in_sem.at[0])
+        lwait(wd, in_sem.at[1])
+        lwait(wo, in_sem.at[2])
+        lwait(wq.at[:, :, pl.ds(0, HL)], in_sem.at[3])
         rwait(wq.at[:, :, pl.ds(HL, HL)], wq_s)
         rwait(wq.at[:, :, pl.ds(HL, HL)], wq_r)
 
@@ -465,7 +467,7 @@
     run((s5, e), (s6, e - 1))
     nxt(s7, s8)
     run((s6, e))
-    nxt(s7, s8, s9a, s7, s8, s9a, s7, s8, s9a)
+    nxt(s7, s8, s9a, s7, s8, s9a, s7, s9a)
     gcp.wait_send()
     rwait(ss1.at[:, pl.ds(0, 3)], ss1_s)
     for k in range(2):
@@ -477,8 +479,20 @@
     for k in range(2):
         rwait(psnd.at[k], p_s.at[k])
 
-    while done[s8] < C:
+    while done[s8] < C - HOLD - 1:
         nxt(s8, s9a)
+    while done[s8] < C - 1:
+        s8(jnp.int32(done[s8]), late=True)
+        done[s8] += 1
+        if done[s9a] < C - HOLD - 1:
+            nxt(s9a)
+
+    s8(jnp.int32(C - 1), late=True)
+
+    @pl.when(c == 1)
+    def _():
+        for i in range(C - HOLD - 1, C):
+            qacopy(jnp.int32(i), 0).start()
 
     rwait(ss2.at[:, pl.ds(0, 3)], ss2_s)
     rwait(nf2.at[:, pl.ds(0, HL)], n2_s)
@@ -526,9 +540,9 @@
             V((3, nh, T, FB), BF16), V((2, T, HL), F32), V((3, T, HL), F32),
             V((C, nh, 1, 128), F32), V((S, 2 * HL), BF16),
             V((C, T, QB), F32), V((C, T, QB), F32), V((C, T, QB), F32),
-            dma((8,)), dma((NB,)), dma, dma, dma, dma((2 * TP,)), dma, dma,
-            dma((3,)), dma((3,)), dma, dma((2,)), dma((2,)), dma((3,)), dma((3, 3)), dma((3, 3)), dma((2,)), dma((3,)),
-            dma, dma((C,)), dma, dma((C,)), dma, dma((C,)), dma, dma((C + 1,)),
+            dma((4,)), dma((NB,)), dma, dma((2,)), dma, dma((2 * TP,)), dma, dma,
+            dma((3,)), dma((3,)), dma, dma((2,)), dma((2,)), dma((3,)), dma((3,)), dma((3, 3)), dma((2,)), dma((3,)),
+            dma, dma((4,)), dma, dma((C,)), dma, dma((C,)), dma, dma((C + 1,)),
         ]
         xo, qo, _ = pl.pallas_call(
             functools.partial(_kernel, T, C, float(d)),

time: 262 us -> 261 us (level)
  no operation moved by 1% of the time
where the time goes in v4:
time: 261 us
  Pallas kernels  260 us (100%)
    pallas_call x1, Pallas kernels, body(): pl.pallas_call(functools.partial(_kernel, T, C, float(d)), out_shape=(V((...  258 us

profile of v4, /device:TPU:0, one launch (start us, length us, event | category | flops | bytes accessed | tf_op | source)
XLA Modules:
  0.0 260.7 jit_solution(905117645075604636)
XLA Ops:
  0.6 257.8 %block.1 = (bf16[512,1024]{1,0:T(8,128)(2,1)S(1)}, bf16[512,3072]{1,0:T(8,128)(2,1)S(1)}, bf16[14,2,1024,256]{3,2,1,0:T(8,128)(2,1)}) custom-call(bf16[512,1024]{1,0:T(8,128)(2,1)} %x_hbm.1, f32[1,1024]{1,0:T(1,128)} %bitcast.2, f32[1,1024]{1,0:T(1,128)} %bitcast.3, bf16[1024,7168]{1,0:T(8,128)(2,1)} %wg_hbm.1, bf16[1024,7168]{1,0:T(8,128)(2,1)} %wu_hbm.1, ...), custom_call_target="tpu_custom_call" | custom-call | tf_op jit(solution)/shard_map/block/pallas_call | solution.py:547
  258.5 2.1 out.1

commit v5 on v4

--- a/solution.py
+++ b/solution.py
@@ -12,7 +12,7 @@
 F32 = jnp.float32
 BF16 = jnp.bfloat16
 NT = 256
-NB = 3
+NB = 4
 HOLD = 2
 
 
@@ -378,6 +378,8 @@
         start_sib(t + 1)
 
     start_sib(jnp.int32(TP + 1))
+    for g in range(TP + 2, TP + NB - 1):
+        prefetch(jnp.int32(g))
     xcopy(1).wait_recv()
     for j in range(1, C):
         norm1(j)

time: 261 us -> 261 us (level)
  no operation moved by 1% of the time
where the time goes in v5:
time: 261 us
  Pallas kernels  260 us (100%)
    pallas_call x1, Pallas kernels, body(): pl.pallas_call(functools.partial(_kernel, T, C, float(d)), out_shape=(V((...  258 us

profile of v5, /device:TPU:0, one launch (start us, length us, event | category | flops | bytes accessed | tf_op | source)
XLA Modules:
  0.0 260.7 jit_solution(6803926738274064375)
XLA Ops:
  0.6 257.9 %block.1 = (bf16[512,1024]{1,0:T(8,128)(2,1)S(1)}, bf16[512,3072]{1,0:T(8,128)(2,1)S(1)}, bf16[14,2,1024,256]{3,2,1,0:T(8,128)(2,1)}) custom-call(bf16[512,1024]{1,0:T(8,128)(2,1)} %x_hbm.1, f32[1,1024]{1,0:T(1,128)} %bitcast.2, f32[1,1024]{1,0:T(1,128)} %bitcast.3, bf16[1024,7168]{1,0:T(8,128)(2,1)} %wg_hbm.1, bf16[1024,7168]{1,0:T(8,128)(2,1)} %wu_hbm.1, ...), custom_call_target="tpu_custom_call" | custom-call | tf_op jit(solution)/shard_map/block/pallas_call | solution.py:549
  258.5 2.1 out.1

commit v6 on v5

--- a/solution.py
+++ b/solution.py
@@ -14,6 +14,7 @@
 NT = 256
 NB = 4
 HOLD = 2
+DIRECT = 16
 
 
 def _dot(a, b):
@@ -25,8 +26,12 @@
             xov, qall, wsib_hbm,
             xv, g1v, g2v, ov, wd, wo, wq, wbuf, nf, ss1, psnd, prcv, pkeep, abuf, ysnd, yrcv, ss2, nf2,
             qsnd, qrcv, qkeep,
-            in_sem, ld_sem, w0_s, w0_r, ws_s, ws_r, wq_s, wq_r, n_s, n_r, ss1_s, ss1_r, p_s, p_r, a_s, a_r, y_s, y_r, ss2_s, ss2_r,
-            n2_s, n2_r, q_s, q_r, qa_s, qa_r):
+            in_sem, ld_sem, w0_s, ws_s, wq_s, ss1_s, p_s, p_r, a_s, a_r, y_s, y_r, ss2_s, ss2_r, n2_s, q_s, qa_s,
+            pool_a, pool_b):
+    ws_r, n2_r, q_r = pool_a, pool_a.at[pl.ds(0, C)], pool_a.at[pl.ds(C, C)]
+    n_s, n_r, w0_r, ss1_r, wq_r = (pool_b.at[pl.ds(0, 3)], pool_b.at[pl.ds(3, 3)], pool_b.at[pl.ds(6, 2)],
+                                   pool_b.at[pl.ds(8, 2)], pool_b.at[10])
+    qa_r = pool_b
     S = xv.shape[0]
     HL = xv.shape[1]
     FB = abuf.shape[3]
@@ -339,11 +344,16 @@
         for t in range(QT):
             qkeep[i, :, t * NT:(t + 1) * NT] = _dot(nn, wq[1, t])
 
-    def qacopy(i, k):
+    def qacopy(i, k, last=False):
         b = (h, h, hx)[k]
         dev = (XP, SIB, SIB)[k]
-        blk = qall.at[pl.ds(mo(i * T, T), T), pl.ds(mo(b * QB, NT), QB)]
-        return rcopy(blk, blk, qa_s, qa_r.at[i if k == 0 else C], dev)
+        n = T - DIRECT if last and k != 1 else T
+        blk = qall.at[pl.ds(mo(i * T, T), n), pl.ds(mo(b * QB, NT), QB)]
+        return rcopy(blk, blk, qa_s, qa_r.at[(i, C, C + 2)[k]], dev)
+
+    def direct(k):
+        blk = qall.at[pl.ds(S - DIRECT, DIRECT), pl.ds(mo(h * QB, NT), QB)]
+        return rcopy(blk, blk, qa_s, qa_r.at[C + 1], (XP, DIAG)[k])
 
     def s8(i, late=False):
         qcopy(i).wait_recv()
@@ -417,6 +427,11 @@
         for j in range(2):
             pkeep[j, t, :, 0:NT] = gg[j * T:(j + 1) * T]
             pkeep[j, t, :, NT:2 * NT] = uu[j * T:(j + 1) * T]
+
+    gcp.wait_send()
+    rwait(ss1.at[:, pl.ds(0, 3)], ss1_s)
+    for k in range(2):
+        xcopy(k).wait_send()
 
     def stage(fn, i, lo=0):
         @pl.when((i >= lo) & (i < C))
@@ -470,11 +485,6 @@
     nxt(s7, s8)
     run((s6, e))
     nxt(s7, s8, s9a, s7, s8, s9a, s7, s9a)
-    gcp.wait_send()
-    rwait(ss1.at[:, pl.ds(0, 3)], ss1_s)
-    for k in range(2):
-        xcopy(k).wait_send()
-
     rwait(wsib_hbm, ws_s)
     rwait(wbuf.at[0, :, pl.ds(HL, HL)], w0_s)
 
@@ -493,16 +503,35 @@
 
     @pl.when(c == 1)
     def _():
-        for i in range(C - HOLD - 1, C):
+        for i in range(C - HOLD - 1, C - 1):
             qacopy(jnp.int32(i), 0).start()
+        qacopy(jnp.int32(C - 1), 0, last=True).start()
+        direct(0).start()
+        direct(1).start()
 
     rwait(ss2.at[:, pl.ds(0, 3)], ss2_s)
     rwait(nf2.at[:, pl.ds(0, HL)], n2_s)
     rwait(qsnd, q_s)
 
-    while done[s9a] < C:
+    while done[s9a] < C - 1:
         nxt(s9a)
-    rwait(qall.at[:, pl.ds(0, 2 * QB)], qa_r.at[C])
+    e = jnp.int32(C - 1)
+    rows = pl.ds(0, DIRECT)
+
+    @pl.when(c == 0)
+    def _():
+        s9a(e)
+        rwait(qall.at[pl.ds(0, S - DIRECT), pl.ds(0, QB)], qa_r.at[C + 2])
+        rwait(qall.at[rows, pl.ds(0, QB)], qa_r.at[C + 1])
+
+    @pl.when(c == 1)
+    def _():
+        qacopy(e, 0, last=True).wait_recv()
+        qacopy(e, 2, last=True).start()
+        rwait(qall.at[:, pl.ds(0, QB)], qa_r.at[C + 2])
+        rwait(qall.at[rows, pl.ds(0, QB)], qa_r.at[C + 1])
+
+    rwait(qall.at[:, pl.ds(0, QB)], qa_r.at[C])
     rwait(qall.at[:, pl.ds(0, 3 * QB)], qa_s)
 
 
@@ -542,9 +571,9 @@
             V((3, nh, T, FB), BF16), V((2, T, HL), F32), V((3, T, HL), F32),
             V((C, nh, 1, 128), F32), V((S, 2 * HL), BF16),
             V((C, T, QB), F32), V((C, T, QB), F32), V((C, T, QB), F32),
-            dma((4,)), dma((NB,)), dma, dma((2,)), dma, dma((2 * TP,)), dma, dma,
-            dma((3,)), dma((3,)), dma, dma((2,)), dma((2,)), dma((3,)), dma((3,)), dma((3, 3)), dma((2,)), dma((3,)),
-            dma, dma((4,)), dma, dma((C,)), dma, dma((C,)), dma, dma((C + 1,)),
+            dma((4,)), dma((NB,)), dma, dma, dma, dma,
+            dma((2,)), dma((3,)), dma((3,)), dma((3, 3)), dma((2,)), dma((3,)), dma, dma((4,)), dma, dma, dma,
+            dma((max(2 * TP, 2 * C),)), dma((C + 3,)),
         ]
         xo, qo, _ = pl.pallas_call(
             functools.partial(_kernel, T, C, float(d)),

time: 261 us -> 261 us (level)
  no operation moved by 1% of the time
where the time goes in v6:
time: 261 us; the launch traced here: 260 us
  Pallas kernels  259 us (99%)
    pallas_call x1, Pallas kernels, body(): pl.pallas_call(functools.partial(_kernel, T, C, float(d)), out_shape=(V((...  257 us

profile of v6, /device:TPU:0, one launch (start us, length us, event | category | flops | bytes accessed | tf_op | source)
XLA Modules:
  0.0 260.2 jit_solution(15846291735797868357)
XLA Ops:
  0.6 257.4 %block.1 = (bf16[512,1024]{1,0:T(8,128)(2,1)S(1)}, bf16[512,3072]{1,0:T(8,128)(2,1)S(1)}, bf16[14,2,1024,256]{3,2,1,0:T(8,128)(2,1)}) custom-call(bf16[512,1024]{1,0:T(8,128)(2,1)} %x_hbm.1, f32[1,1024]{1,0:T(1,128)} %bitcast.2, f32[1,1024]{1,0:T(1,128)} %bitcast.3, bf16[1024,7168]{1,0:T(8,128)(2,1)} %wg_hbm.1, bf16[1024,7168]{1,0:T(8,128)(2,1)} %wu_hbm.1, ...), custom_call_target="tpu_custom_call" | custom-call | tf_op jit(solution)/shard_map/block/pallas_call | solution.py:578
  258.0 2.1 out.1

commit v7 on v6

--- a/solution.py
+++ b/solution.py
@@ -228,7 +228,7 @@
         psnd[s2, t, :, NT:2 * NT] = uu
         pcopy(j, t).start()
 
-    def s12(j):
+    def s12(j, between):
         s2 = lax.rem(j, 2)
         g0 = 3 * TP + (j - 2) * (2 * TP)
         rwait(psnd.at[s2], p_s.at[s2])
@@ -249,6 +249,10 @@
             pkeep[s2, t, :, 0:NT] = gg
             pkeep[s2, t, :, NT:2 * NT] = uu
 
+            @pl.when(t < DT)
+            def _():
+                between(t)
+
     def acopy(i, k):
         sl = lax.rem(i, 3)
         b = (h, h, hx)[k]
@@ -278,17 +282,20 @@
     def down(sl, b, n):
         return _dot(abuf[sl, b], wd[n, pl.ds(mo(b * FB, FB), FB)])
 
-    def s4a(i):
+    def down_own(i, n):
         s2 = lax.rem(i, 2)
         sl = lax.rem(i, 3)
+        acc = _dot(ov[pl.ds(mo(i * T, T), T), :], wo[n])
+        acc += down(sl, h, n)
+        acc += down(sl, hs, n)
+        ysnd[s2, :, pl.ds(mo(n * NT, NT), NT)] = acc
+
+    def s4a(i):
         acopy(i, 1).wait_recv()
 
         @pl.loop(0, DT)
         def _(n):
-            acc = _dot(ov[pl.ds(mo(i * T, T), T), :], wo[n])
-            acc += down(sl, h, n)
-            acc += down(sl, hs, n)
-            ysnd[s2, :, pl.ds(mo(n * NT, NT), NT)] = acc
+            down_own(i, n)
 
     def s4b(i):
         s2 = lax.rem(i, 2)
@@ -449,14 +456,20 @@
     @pl.loop(0, C - 2)
     def _(i):
         s3(i)
-        s12(i + 2)
 
         @pl.when(i == 0)
         def _():
             loaded()
 
+        def between(n):
+            @pl.when(n == 0)
+            def _():
+                acopy(i, 1).wait_recv()
+
+            down_own(i, n)
+
+        s12(i + 2, between)
         stage(s5, i - 1)
-        s4a(i)
         s4b(i)
         stage(s6, i - 2)
 
@@ -537,12 +550,12 @@
 
 def _out_kernel(xv, qv, xo, qo, sem):
     n = xv.shape[0] // 4
-    cps = [pltpu.make_async_copy(a.at[pl.ds(k * n, n)], b.at[pl.ds(k * n, n)], sem.at[m, k])
+    cps = [pltpu.make_async_copy(a.at[pl.ds(k * n, n)], b.at[pl.ds(k * n, n)], sem.at[m])
            for m, (a, b) in enumerate(((qv, qo), (xv, xo))) for k in range(4)]
     for cp in cps:
         cp.start()
-    for cp in cps:
-        cp.wait()
+    for m, (a, b) in enumerate(((qv, qo), (xv, xo))):
+        pltpu.make_async_copy(a, b, sem.at[m]).wait()
 
 
 def solution(mesh):
@@ -589,7 +602,7 @@
             out_shape=(jax.ShapeDtypeStruct((S, HL), BF16), jax.ShapeDtypeStruct((S, QL), BF16)),
             in_specs=[vm, vm],
             out_specs=(any_, any_),
-            scratch_shapes=[dma((2, 4))],
+            scratch_shapes=[dma((2,))],
             compiler_params=pltpu.CompilerParams(vmem_limit_bytes=2**20),
             name='out',
         )(xo, qo)

time: 261 us -> 261 us (level)
  no operation moved by 1% of the time
where the time goes in v7:
time: 261 us; the launch traced here: 260 us
  Pallas kernels  259 us (99%)
    pallas_call x1, Pallas kernels, body(): pl.pallas_call(functools.partial(_kernel, T, C, float(d)), out_shape=(V((...  257 us

profile of v7, /device:TPU:0, one launch (start us, length us, event | category | flops | bytes accessed | tf_op | source)
XLA Modules:
  0.0 260.2 jit_solution(11344291691133806294)
XLA Ops:
  0.6 257.4 %block.1 = (bf16[512,1024]{1,0:T(8,128)(2,1)S(1)}, bf16[512,3072]{1,0:T(8,128)(2,1)S(1)}, bf16[14,2,1024,256]{3,2,1,0:T(8,128)(2,1)}) custom-call(bf16[512,1024]{1,0:T(8,128)(2,1)} %x_hbm.1, f32[1,1024]{1,0:T(1,128)} %bitcast.2, f32[1,1024]{1,0:T(1,128)} %bitcast.3, bf16[1024,7168]{1,0:T(8,128)(2,1)} %wg_hbm.1, bf16[1024,7168]{1,0:T(8,128)(2,1)} %wu_hbm.1, ...), custom_call_target="tpu_custom_call" | custom-call | tf_op jit(solution)/shard_map/block/pallas_call | solution.py:591
  258.0 2.0 out.1

commit v8 on v7

--- a/solution.py
+++ b/solution.py
@@ -26,12 +26,13 @@
             xov, qall, wsib_hbm,
             xv, g1v, g2v, ov, wd, wo, wq, wbuf, nf, ss1, psnd, prcv, pkeep, abuf, ysnd, yrcv, ss2, nf2,
             qsnd, qrcv, qkeep,
-            in_sem, ld_sem, w0_s, ws_s, wq_s, ss1_s, p_s, p_r, a_s, a_r, y_s, y_r, ss2_s, ss2_r, n2_s, q_s, qa_s,
+            in_sem, ld_sem, w0_s, ws_s, wq_s, ss1_s, p_s, p_r, a_s, a_r, y_s, y_r, ss2_r,
             pool_a, pool_b):
     ws_r, n2_r, q_r = pool_a, pool_a.at[pl.ds(0, C)], pool_a.at[pl.ds(C, C)]
     n_s, n_r, w0_r, ss1_r, wq_r = (pool_b.at[pl.ds(0, 3)], pool_b.at[pl.ds(3, 3)], pool_b.at[pl.ds(6, 2)],
                                    pool_b.at[pl.ds(8, 2)], pool_b.at[10])
     qa_r = pool_b
+    ss2_s, n2_s, q_s, qa_s = ss1_s, ws_s, wq_s, w0_s
     S = xv.shape[0]
     HL = xv.shape[1]
     FB = abuf.shape[3]
@@ -452,6 +453,8 @@
         lwait(wq.at[:, :, pl.ds(0, HL)], in_sem.at[3])
         rwait(wq.at[:, :, pl.ds(HL, HL)], wq_s)
         rwait(wq.at[:, :, pl.ds(HL, HL)], wq_r)
+        rwait(wsib_hbm, ws_s)
+        rwait(wbuf.at[0, :, pl.ds(HL, HL)], w0_s)
 
     @pl.loop(0, C - 2)
     def _(i):
@@ -498,8 +501,6 @@
     nxt(s7, s8)
     run((s6, e))
     nxt(s7, s8, s9a, s7, s8, s9a, s7, s9a)
-    rwait(wsib_hbm, ws_s)
-    rwait(wbuf.at[0, :, pl.ds(HL, HL)], w0_s)
 
     for k in range(2):
         rwait(psnd.at[k], p_s.at[k])
@@ -585,7 +586,7 @@
             V((C, nh, 1, 128), F32), V((S, 2 * HL), BF16),
             V((C, T, QB), F32), V((C, T, QB), F32), V((C, T, QB), F32),
             dma((4,)), dma((NB,)), dma, dma, dma, dma,
-            dma((2,)), dma((3,)), dma((3,)), dma((3, 3)), dma((2,)), dma((3,)), dma, dma((4,)), dma, dma, dma,
+            dma((2,)), dma((3,)), dma((3,)), dma((3, 3)), dma((2,)), dma((3,)), dma((4,)),
             dma((max(2 * TP, 2 * C),)), dma((C + 3,)),
         ]
         xo, qo, _ = pl.pallas_call(

time: 261 us -> 260 us (level)
  no operation moved by 1% of the time
where the time goes in v8:
time: 260 us
  Pallas kernels  259 us (100%)
    pallas_call x1, Pallas kernels, body(): pl.pallas_call(functools.partial(_kernel, T, C, float(d)), out_shape=(V((...  257 us

profile of v8, /device:TPU:0, one launch (start us, length us, event | category | flops | bytes accessed | tf_op | source)
XLA Modules:
  0.0 260.1 jit_solution(9075060129994011850)
XLA Ops:
  0.6 257.3 %block.1 = (bf16[512,1024]{1,0:T(8,128)(2,1)S(1)}, bf16[512,3072]{1,0:T(8,128)(2,1)S(1)}, bf16[14,2,1024,256]{3,2,1,0:T(8,128)(2,1)}) custom-call(bf16[512,1024]{1,0:T(8,128)(2,1)} %x_hbm.1, f32[1,1024]{1,0:T(1,128)} %bitcast.2, f32[1,1024]{1,0:T(1,128)} %bitcast.3, bf16[1024,7168]{1,0:T(8,128)(2,1)} %wg_hbm.1, bf16[1024,7168]{1,0:T(8,128)(2,1)} %wu_hbm.1, ...), custom_call_target="tpu_custom_call" | custom-call | tf_op jit(solution)/shard_map/block/pallas_call | solution.py:592
  258.0 2.0 out.1
